TPU v7x, 32 devices: a whole 2x2x4 slice. The times are simulated.
32 devices in a mesh: dp: 8 (over z, y), seq: 4 (over x, core).
Axes of the slice: x: 2, y: 2, z: 4, core: 2. Of those that a mesh axis runs over, the one named last changes fastest.
Arguments:
- inputs: bfloat16 [48, 1024, 256], P('dp', 'seq')
- cotangent: bfloat16 [48, 1024, 256], P('dp', 'seq')
- owner_list: int32 [7], replicated, may hold values from 0 to 7, as said below
- master_rows: float32 [8, 524288], P('dp'), as said below
- moment1_rows: float32 [8, 524288], P('dp'), as said below
- moment2_rows: float32 [8, 524288], P('dp'), as said below
Outputs:
- final_state: float32 [48, 1024, 256], P('dp', 'seq')
- input_grad: float32 [48, 1024, 256], P('dp', 'seq')
- state_stats: float32 [2, 48], replicated
- new_moment1: float32 [8, 524288], P('dp')
- new_moment2: float32 [8, 524288], P('dp')
- new_master: float32 [8, 524288], P('dp')
Inputs may be any that keep to these rules, and one draw needn't show every extreme that they name: Tensor t goes to dp index owner_list[t]. W_up and W_down share one owner that holds no other tensor, so the busiest owner holds 524288 entries; the other five tensors are dealt among the other indices, several may share one. `master_rows`: entries of a row beyond the tensors its owner holds are not read. `moment1_rows`: entries of a row beyond the tensors its owner holds are not read. `moment2_rows`: Positive. Entries beyond the tensors an owner holds are not read.
All inputs are finite; a program needn't handle non-finite values.
Results may differ from a plain program's by a relative error of at most 0.02.
The roundings to bfloat16 on the way count: a program that leaves them out, or rounds other values in their place, can miss the bound.
Values may be sent and summed in bfloat16 or wider, within the bound.
A program may use at most 192 MiB of HBM per device.

v0:
```python
from functools import partial
import jax
import jax.numpy as jnp
from jax import lax
from jax.sharding import PartitionSpec as P

D = 256
HEADS = 4
HD = 64
FF = 1024
STEP = 3
SMALL = 9
norm_eps = 1e-05
stat_eps = 1e-06
adam_eps = 1e-08
masked_score = -1e30


def tensor_shapes():
    return [(D, D), (D, D), (D, D), (D, D), (D, FF), (FF, D), (SMALL, D)]


def owner_starts(owner_list):
    shapes = tensor_shapes()
    starts = []
    for tensor_id in range(7):
        offset = jnp.zeros((), jnp.int32)
        for earlier in range(tensor_id):
            shared = (owner_list[earlier] == owner_list[tensor_id]).astype(jnp.int32)
            offset = offset + shared * (shapes[earlier][0] * shapes[earlier][1])
        starts.append(offset)
    return starts


def layer_norm(values, norm_gain, norm_shift):
    average = jnp.mean(values, axis=-1, keepdims=True)
    centered = values - average
    spread = jnp.mean(centered * centered, axis=-1, keepdims=True)
    return centered * lax.rsqrt(spread + norm_eps) * norm_gain + norm_shift


def masked_scores(packed):
    length = packed.shape[0]
    queries = packed[:, :, :HD]
    keys_part = packed[:, :, HD : 2 * HD]
    scores = jnp.einsum(
        "qhd,khd->hqk", queries, keys_part, preferred_element_type=jnp.float32
    ) * HD ** (-0.5)
    causal = lax.broadcasted_iota(jnp.int32, (length, length), 0) >= lax.broadcasted_iota(
        jnp.int32, (length, length), 1
    )
    return jnp.where(causal[None], scores, masked_score)


def attend_single(packed):
    scores = masked_scores(packed)
    highest_score = jnp.max(scores, axis=-1, keepdims=True)
    raw_weights = jnp.exp(scores - highest_score)
    totals = jnp.sum(raw_weights, axis=-1, keepdims=True)
    attention_probs = raw_weights / totals
    values_part = packed[:, :, 2 * HD :]
    attention_output = jnp.einsum(
        "hqk,khd->qhd",
        attention_probs.astype(jnp.bfloat16),
        values_part,
        preferred_element_type=jnp.float32,
    )
    return (attention_output.astype(jnp.bfloat16), (highest_score + jnp.log(totals))[..., 0])


def attend_items(packed_items):
    attention_output, log_total = lax.map(attend_single, packed_items)
    return (attention_output, log_total, packed_items)


def attend_single_back(parts):
    packed, log_total, grad_attended = parts
    queries = packed[:, :, :HD]
    keys_part = packed[:, :, HD : 2 * HD]
    values_part = packed[:, :, 2 * HD :]
    scores = masked_scores(packed)
    attention_probs = jnp.exp(scores - log_total[..., None])
    grad_probs = jnp.einsum(
        "qhd,khd->hqk", grad_attended, values_part, preferred_element_type=jnp.float32
    )
    inner_sum = jnp.sum(attention_probs * grad_probs, axis=-1, keepdims=True)
    grad_scores = (attention_probs * (grad_probs - inner_sum)).astype(jnp.bfloat16)
    grad_queries = jnp.einsum(
        "hqk,khd->qhd", grad_scores, keys_part, preferred_element_type=jnp.float32
    ) * HD ** (-0.5)
    grad_keys = jnp.einsum(
        "hqk,qhd->khd", grad_scores, queries, preferred_element_type=jnp.float32
    ) * HD ** (-0.5)
    grad_values = jnp.einsum(
        "hqk,qhd->khd",
        attention_probs.astype(jnp.bfloat16),
        grad_attended,
        preferred_element_type=jnp.float32,
    )
    return jnp.concatenate([grad_queries, grad_keys, grad_values], axis=-1).astype(jnp.bfloat16)


def block_forward(loop_state, combined_weight, output_weight, up_weight, down_weight, small_piece):
    seq_count, quarter, features = loop_state.shape
    normalized_input = layer_norm(loop_state, small_piece[0], small_piece[1]).astype(jnp.bfloat16)
    projected = jnp.einsum(
        "fur,rk->fuk", normalized_input, combined_weight, preferred_element_type=jnp.float32
    ).astype(jnp.bfloat16)
    per_head = projected.reshape(seq_count, quarter, HEADS, 3 * HD)
    head_out, log_total, packed = attend_items(
        lax.all_to_all(per_head, "seq", split_axis=2, concat_axis=1, tiled=True)
    )
    attention_output = lax.all_to_all(
        head_out, "seq", split_axis=1, concat_axis=2, tiled=True
    ).reshape(seq_count, quarter, features)
    middle_state = loop_state + jnp.einsum(
        "fur,rk->fuk", attention_output, output_weight, preferred_element_type=jnp.float32
    )
    normalized_middle = layer_norm(middle_state, small_piece[2], small_piece[3]).astype(
        jnp.bfloat16
    )
    before = jnp.einsum(
        "sgm,mk->sgk", normalized_middle, up_weight, preferred_element_type=jnp.float32
    ) + small_piece[5:].reshape(FF)
    hidden_units = jax.nn.gelu(before, approximate=False).astype(jnp.bfloat16)
    result = middle_state + (
        jnp.einsum("czm,mg->czg", hidden_units, down_weight, preferred_element_type=jnp.float32)
        + small_piece[4]
    )
    saved = (
        loop_state,
        normalized_input,
        packed,
        log_total,
        attention_output,
        middle_state,
        normalized_middle,
        before,
        hidden_units,
    )
    return (result, saved)


def block_backward(
    grad_result, saved, combined_weight, output_weight, up_weight, down_weight, small_piece
):
    (
        loop_state,
        normalized_input,
        packed,
        log_total,
        attention_output,
        middle_state,
        normalized_middle,
        before,
        hidden_units,
    ) = saved
    seq_count, quarter, features = loop_state.shape
    branch_gradient = grad_result.astype(jnp.bfloat16)
    down_gradient = jnp.einsum(
        "yeo,yen->on", hidden_units, branch_gradient, preferred_element_type=jnp.float32
    )
    grad_bias_down = jnp.sum(branch_gradient.astype(jnp.float32), axis=(0, 1))
    hidden_gradient = jnp.einsum(
        "vel,kl->vek", branch_gradient, down_weight, preferred_element_type=jnp.float32
    )
    gelu_pull = jax.vjp(partial(jax.nn.gelu, approximate=False), before)[1]
    gradient_prior = gelu_pull(hidden_gradient)[0].astype(jnp.bfloat16)
    up_gradient = jnp.einsum(
        "erv,erh->vh", normalized_middle, gradient_prior, preferred_element_type=jnp.float32
    )
    grad_bias_up = jnp.sum(gradient_prior.astype(jnp.float32), axis=(0, 1))
    grad_normed_mid = jnp.einsum(
        "tam,em->tae", gradient_prior, up_weight, preferred_element_type=jnp.float32
    )
    second_pull = jax.vjp(layer_norm, middle_state, small_piece[2], small_piece[3])[1]
    grad_mid_part, grad_gain_two, grad_shift_two = second_pull(grad_normed_mid)
    grad_middle = grad_result + grad_mid_part
    attention_gradient = grad_middle.astype(jnp.bfloat16)
    grad_out_weight = jnp.einsum(
        "tck,tcp->kp", attention_output, attention_gradient, preferred_element_type=jnp.float32
    )
    grad_attended = jnp.einsum(
        "tkh,nh->tkn", attention_gradient, output_weight, preferred_element_type=jnp.float32
    ).astype(jnp.bfloat16)
    grad_heads = lax.all_to_all(
        grad_attended.reshape(seq_count, quarter, HEADS, HD),
        "seq",
        split_axis=2,
        concat_axis=1,
        tiled=True,
    )
    grad_packed = lax.map(attend_single_back, (packed, log_total, grad_heads))
    projected_gradient = lax.all_to_all(
        grad_packed, "seq", split_axis=1, concat_axis=2, tiled=True
    ).reshape(seq_count, quarter, 3 * features)
    grad_joined = jnp.einsum(
        "tck,tcp->kp", normalized_input, projected_gradient, preferred_element_type=jnp.float32
    )
    grad_normed = jnp.einsum(
        "tkh,nh->tkn", projected_gradient, combined_weight, preferred_element_type=jnp.float32
    )
    first_pull = jax.vjp(layer_norm, loop_state, small_piece[0], small_piece[1])[1]
    grad_state_part, grad_gain_one, grad_shift_one = first_pull(grad_normed)
    grad_state = grad_middle + grad_state_part
    grad_small = jnp.concatenate(
        [
            jnp.stack(
                [grad_gain_one, grad_shift_one, grad_gain_two, grad_shift_two, grad_bias_down]
            ),
            grad_bias_up.reshape(FF // D, D),
        ],
        axis=0,
    )
    return (grad_state, (grad_joined, grad_out_weight, up_gradient, down_gradient, grad_small))


def gather_stat(square_sums):
    return lax.all_gather(square_sums, ("dp", "seq"), axis=1, tiled=True)


def finish_stats(gathered, entries_total):
    loop_count = gathered.shape[0]
    folded = gathered.reshape(loop_count, lax.axis_size("dp"), lax.axis_size("seq"), -1)
    folded = jnp.sum(folded, axis=2).reshape(loop_count, -1)
    return jnp.sqrt(folded / entries_total + stat_eps)


def split_joined(grad_joined):
    arranged = grad_joined.reshape(D, HEADS, 3, HD)
    return [arranged[:, :, slot_id, :].reshape(D, D) for slot_id in range(3)]


def per_device(inputs, cotangent, owner_list, master_rows, moment1_rows, moment2_rows):
    shapes = tensor_shapes()
    starts = owner_starts(owner_list)
    device_row = lax.axis_index("dp")
    zero_row = jnp.zeros((), jnp.int32)
    owned_parts = []
    for tensor_id in range(7):
        entries = shapes[tensor_id][0] * shapes[tensor_id][1]
        sliced = lax.dynamic_slice(
            master_rows, (zero_row, starts[tensor_id]), (1, entries)
        ).reshape(shapes[tensor_id])
        is_owner = owner_list[tensor_id] == device_row
        owned_parts.append(jnp.where(is_owner, sliced, 0.0))
    masters = lax.psum(
        (
            owned_parts[0],
            owned_parts[1],
            owned_parts[2],
            owned_parts[3],
            owned_parts[4],
            owned_parts[5],
            owned_parts[6],
        ),
        "dp",
    )
    small_piece = masters[6]
    matrices = [matrix.astype(jnp.bfloat16) for matrix in masters[:6]]
    query_low, key_low, value_low, out_low, up_low, down_low = matrices
    combined_weight = jnp.stack(
        [
            query_low.reshape(D, HEADS, HD),
            key_low.reshape(D, HEADS, HD),
            value_low.reshape(D, HEADS, HD),
        ],
        axis=2,
    ).reshape(D, 3 * D)
    start_state = inputs.astype(jnp.float32)
    seq_count, quarter, features = start_state.shape
    entries_total = quarter * lax.axis_size("seq") * features
    first_out, first_saved = block_forward(
        start_state, combined_weight, out_low, up_low, down_low, small_piece
    )
    first_squares = jnp.sum(first_out * first_out, axis=(1, 2))
    first_gathered = gather_stat(first_squares[None])
    second_out, second_saved = block_forward(
        first_out + start_state, combined_weight, out_low, up_low, down_low, small_piece
    )
    second_squares = jnp.sum(second_out * second_out, axis=(1, 2))
    second_gathered = gather_stat(second_squares[None])
    gathered = jnp.concatenate([first_gathered, second_gathered], axis=0)
    state_stats = finish_stats(gathered, entries_total)
    grad_second_in, grads_two = block_backward(
        cotangent.astype(jnp.float32),
        second_saved,
        combined_weight,
        out_low,
        up_low,
        down_low,
        small_piece,
    )
    grad_first_in, grads_one = block_backward(
        grad_second_in, first_saved, combined_weight, out_low, up_low, down_low, small_piece
    )
    local_sums = [part_two + part_one for part_two, part_one in zip(grads_two, grads_one)]
    summed = lax.psum(
        (local_sums[0], local_sums[1], local_sums[2], local_sums[3], local_sums[4]), ("dp", "seq")
    )
    input_grad = grad_second_in + grad_first_in
    gradients = split_joined(summed[0]) + [summed[1], summed[2], summed[3], summed[4]]
    learning_rates = [D ** (-0.5)] * 5 + [FF ** (-0.5), 0.5]
    decays_list = [0.1] * 6 + [0.0]
    correction = 1.0 - 0.5**STEP
    new_moment1 = jnp.zeros_like(moment1_rows)
    new_moment2 = jnp.zeros_like(moment2_rows)
    new_master = jnp.zeros_like(master_rows)
    for tensor_id in range(7):
        entries = shapes[tensor_id][0] * shapes[tensor_id][1]
        corner = (zero_row, starts[tensor_id])
        is_owner = owner_list[tensor_id] == device_row
        gradient = gradients[tensor_id].reshape(1, entries)
        old_first = lax.dynamic_slice(moment1_rows, corner, (1, entries))
        old_second = lax.dynamic_slice(moment2_rows, corner, (1, entries))
        old_weight = lax.dynamic_slice(master_rows, corner, (1, entries))
        first_new = 0.5 * old_first + 0.5 * gradient
        second_new = 0.5 * old_second + 0.5 * gradient * gradient
        update = (
            first_new / correction / (jnp.sqrt(second_new / correction) + adam_eps)
            + decays_list[tensor_id] * old_weight
        )
        weight_new = old_weight - learning_rates[tensor_id] * update
        new_moment1 = lax.dynamic_update_slice(
            new_moment1,
            jnp.where(is_owner, first_new, lax.dynamic_slice(new_moment1, corner, (1, entries))),
            corner,
        )
        new_moment2 = lax.dynamic_update_slice(
            new_moment2,
            jnp.where(is_owner, second_new, lax.dynamic_slice(new_moment2, corner, (1, entries))),
            corner,
        )
        new_master = lax.dynamic_update_slice(
            new_master,
            jnp.where(is_owner, weight_new, lax.dynamic_slice(new_master, corner, (1, entries))),
            corner,
        )
    return (second_out, input_grad, state_stats, new_moment1, new_moment2, new_master)


def solution(mesh):
    placed = (
        P("dp", "seq", None),
        P("dp", "seq", None),
        P(),
        P("dp", None),
        P("dp", None),
        P("dp", None),
    )
    return jax.shard_map(
        per_device,
        mesh=mesh,
        in_specs=placed,
        out_specs=(
            P("dp", "seq", None),
            P("dp", "seq", None),
            P(),
            P("dp", None),
            P("dp", None),
            P("dp", None),
        ),
        check_vma=False,
    )
```

profile of v0, /device:TPU:0, one launch (start us, length us, event | category | flops | bytes accessed | tf_op | source)
XLA Modules:
  0.0 949.5 jit_solution(13561079497772902134)
XLA Ops:
  40.8 13.1 %fusion.104 = (f32[262144]{0:T(1024)S(1)}, f32[262144]{0:T(1024)}) fusion(pred[]{:T(512)S(6)} %eq.113, f32[1,524288]{1,0:T(1,128)} %param.17, s32[]{:T(128)S(6)} %select_n.271, s32[]{:T(128)S(6)} %select_n.267, pred[]{:T(512)S(6)} %eq.108), kind=kLoop, calls=%fused_computation.227 | loop fusion | flops 524288 | bytes 4194314 | tf_op jit(solution)/shard_map/jit(_where)/select_n | solution.py:246
  59.3 3.5 fusion.134
  69.9 132.7 %all-reduce.12 = (bf16[256,256]{1,0:T(8,128)(2,1)S(1)}, bf16[256,256]{1,0:T(8,128)(2,1)S(1)}, bf16[256,256]{1,0:T(8,128)(2,1)S(1)}, f32[9,256]{1,0:T(8,128)S(1)}...) all-reduce(f32[256,256]{1,0:T(8,128)} %select_n.261, ...), channel_id=1, replica_groups=mesh['dp'=8,'seq'=4] {'dp'}, use_global_device_ids=true, to_apply=%region_5.6 | all-reduce | flops 788736 | bytes 4737024 | tf_op jit(solution)/shard_map/psum | solution.py:247
  206.1 4.3 copy.262
  210.4 3.3 copy.263
  213.7 4.5 all-to-all-start
  218.2 28.5 %all-to-all-done = bf16[6,256,4,192]{1,3,0,2:T(8,128)(2,1)} async-done(((bf16[6,256,4,192]{1,3,0,2:T(8,128)(2,1)}), bf16[6,256,4,192]{1,3,0,2:T(8,128)(2,1)}, u32[]{:S(2)}, u32[]{:S(2)}) %all-to-all-start) | async-done | bytes 2359328 | tf_op jit(solution)/shard_map/all_to_all | solution.py:111
  246.7 3.4 copy.374
  250.2 18.3 %while.44 = (s32[]{:T(128)}, bf16[6,1024,1,64]{1,3,2,0:T(8,128)(2,1)S(1)}, f32[6,1,1024]{2,1,0:T(1,128)S(1)}, bf16[6,1024,1,192]{1,3,2,0:T(8,128)(2,1)}, s32[]{:T(128)}) while((s32[]{:T(128)}, bf16[6,1024,1,64]{1,3,2,0:T(8,128)(2,1)S(1)}, f32[6,1,1024]{2,1,0:T(1,128)S(1)}, bf16[6,1024,1,192]{1,3,2,0:T(8,128)(2,1)}, s32[]{:T(128)}) %tuple.165), condition=%wide.region_9.10_spmd, body=%wide.region_6.9_spmd.sunk | while | flops 284228608 | bytes 13934665 | solution.py:72
  268.5 2.5 copy.266
  271.0 4.2 reshape.839
  275.2 3.9 all-to-all-start.1
  279.2 11.5 %all-to-all-done.1 = bf16[4,2,49152]{2,1,0:T(2,128)(2,1)S(1)} async-done(((bf16[4,2,49152]{2,1,0:T(2,128)(2,1)}), bf16[4,2,49152]{2,1,0:T(2,128)(2,1)S(1)}, u32[]{:S(2)}, u32[]{:S(2)}) %all-to-all-start.1) | async-done | bytes 786464 | tf_op jit(solution)/shard_map/all_to_all | solution.py:113
  290.7 2.5 reshape.840
  293.2 2.6 copy.362
  298.0 2.9 fusion.88
  300.9 15.2 %multiply_convert_fusion.3 = (bf16[6,256,1024]{2,1,0:T(8,128)(2,1)S(1)}, f32[6,256,1024]{2,1,0:T(8,128)}) fusion(f32[6,256,1024]{2,1,0:T(8,128)S(1)} %get-tuple-element.342, f32[1024]{0:T(1024)S(1)} %bitcast.501, u8[256,1024]{1,0:T(8,128)(4,1)S(1)} %get-tuple-element.217, u8[256,1024]{1,0:T(8,128)(4,1)S(1)} %get-tuple-element.216), kind=kLoop, calls=%fused_computation.130 | loop fusion | flops 111673344 | bytes 16257024 | tf_op jit(solution)/shard_map/convert_element_type | solution.py:125
  318.4 2.4 convolution_convert_fusion
  320.7 4.3 copy.275
  325.1 3.3 copy.276
  328.4 4.5 all-to-all-start.2
  332.9 28.5 %all-to-all-done.2 = bf16[6,256,4,192]{1,3,0,2:T(8,128)(2,1)} async-done(((bf16[6,256,4,192]{1,3,0,2:T(8,128)(2,1)}), bf16[6,256,4,192]{1,3,0,2:T(8,128)(2,1)}, u32[]{:S(2)}, u32[]{:S(2)}) %all-to-all-start.2) | async-done | bytes 2359328 | tf_op jit(solution)/shard_map/all_to_all | solution.py:111
  361.4 3.4 copy.375
  364.9 18.3 %while.45 = (s32[]{:T(128)}, bf16[6,1024,1,64]{1,3,2,0:T(8,128)(2,1)S(1)}, f32[6,1,1024]{2,1,0:T(1,128)S(1)}, bf16[6,1024,1,192]{1,3,2,0:T(8,128)(2,1)}, s32[]{:T(128)}) while((s32[]{:T(128)}, bf16[6,1024,1,64]{1,3,2,0:T(8,128)(2,1)S(1)}, f32[6,1,1024]{2,1,0:T(1,128)S(1)}, bf16[6,1024,1,192]{1,3,2,0:T(8,128)(2,1)}, s32[]{:T(128)}) %tuple.167), condition=%wide.region_20.21_spmd, body=%wide.region_17.20_spmd.sunk | while | flops 284228608 | bytes 13934665 | solution.py:72
  383.3 2.5 copy.279
  385.8 4.3 reshape.841
  390.1 3.7 all-to-all-start.3
  394.9 10.4 %all-to-all-done.3 = bf16[4,2,49152]{2,1,0:T(2,128)(2,1)S(1)} async-done(((bf16[4,2,49152]{2,1,0:T(2,128)(2,1)}), bf16[4,2,49152]{2,1,0:T(2,128)(2,1)S(1)}, u32[]{:S(2)}, u32[]{:S(2)}) %all-to-all-start.3) | async-done | bytes 786464 | tf_op jit(solution)/shard_map/all_to_all | solution.py:113
  405.3 2.5 reshape.842
  407.8 2.6 copy.364
  412.6 2.9 fusion.89
  415.5 15.1 %multiply_convert_fusion.2 = (bf16[6,256,1024]{2,1,0:T(8,128)(2,1)}, f32[6,256,1024]{2,1,0:T(8,128)S(1)}) fusion(f32[6,256,1024]{2,1,0:T(8,128)S(1)} %get-tuple-element.345, f32[1024]{0:T(1024)S(1)} %bitcast.503, u8[256,1024]{1,0:T(8,128)(4,1)S(1)} %get-tuple-element.215, u8[256,1024]{1,0:T(8,128)(4,1)S(1)} %get-tuple-element.214), kind=kLoop, calls=%fused_computation.117 | loop fusion | flops 111673344 | bytes 16257024 | tf_op jit(solution)/shard_map/convert_element_type | solution.py:125
  430.6 3.4 convert_reduce_fusion.1
  436.2 3.0 copy.288
  444.4 4.4 all-to-all-start.4
  448.9 11.7 %all-to-all-done.4 = bf16[6,256,4,64]{1,3,0,2:T(8,128)(2,1)} async-done(((bf16[6,256,4,64]{1,3,0,2:T(8,128)(2,1)}), bf16[6,256,4,64]{1,3,0,2:T(8,128)(2,1)}, u32[]{:S(2)}, u32[]{:S(2)}) %all-to-all-start.4) | async-done | bytes 786464 | tf_op jit(solution)/shard_map/all_to_all | solution.py:186
  464.3 52.6 %while.46 = (s32[]{:T(128)}, bf16[6,1024,1,192]{1,3,2,0:T(8,128)(2,1)}, bf16[6,1024,1,192]{1,3,2,0:T(8,128)(2,1)}, f32[6,1,1024]{2,1,0:T(1,128)S(1)}, bf16[6,1024,1,64]{1,3,2,0:T(8,128)(2,1)}, /*index=5*/s32[]{:T(128)}) while((s32[]{:T(128)}, bf16[6,1024,1,192]{1,3,2,0:T(8,128)(2,1)}, bf16[6,1024,1,192]{1,3,2,0:T(8,128)(2,1)}, ...), condition=%wide.region_27.28_spmd, body=%wide.region_25.27_spmd.sunk | while | flops 683080704 | bytes 34362956 | solution.py:193
  516.9 6.6 copy.295
  523.5 53.8 %all_to_all.132 = bf16[6,1024,1,192]{3,0,2,1:T(8,128)(2,1)} all-to-all(bf16[6,1024,1,192]{3,0,2,1:T(8,128)(2,1)} %copy.295), channel_id=1, replica_groups=mesh['dp'=8,'seq'=4] {'seq'}, dimensions={1} | all-to-all | bytes 4718592 | tf_op jit(solution)/shard_map/all_to_all | solution.py:194
  577.3 5.6 copy.368
  587.1 3.0 copy.300
  594.6 7.0 convert_reduce_fusion
  603.8 3.0 copy.303
  606.9 2.5 multiply_reduce_fusion.2
  613.3 4.6 all-to-all-start.6
  618.1 4.2 multiply_reduce_fusion.5
  622.3 3.0 copy.331
  625.5 4.0 all-to-all-done.6
  633.3 56.6 %while.47 = (s32[]{:T(128)}, bf16[6,1024,1,192]{1,3,2,0:T(8,128)(2,1)}, bf16[6,1024,1,192]{1,3,2,0:T(8,128)(2,1)}, f32[6,1,1024]{2,1,0:T(1,128)}, bf16[6,1024,1,64]{1,3,2,0:T(8,128)(2,1)}, /*index=5*/s32[]{:T(128)}) while((s32[]{:T(128)}, bf16[6,1024,1,192]{1,3,2,0:T(8,128)(2,1)}, bf16[6,1024,1,192]{1,3,2,0:T(8,128)(2,1)}, ...), condition=%wide.region_34.35_spmd, body=%wide.region_32.34_spmd.sunk | while | flops 683080704 | bytes 34362956 | solution.py:193
  689.9 6.5 copy.310
  696.4 4.9 all-to-all-start.7
  701.6 3.5 convolution_bitcast_fusion
  715.5 34.0 %all-to-all-done.7 = bf16[6,1024,1,192]{3,0,2,1:T(8,128)(2,1)} async-done(((bf16[6,1024,1,192]{3,0,2,1:T(8,128)(2,1)}), bf16[6,1024,1,192]{3,0,2,1:T(8,128)(2,1)}, u32[]{:S(2)}, u32[]{:S(2)}) %all-to-all-start.7) | async-done | bytes 2359328 | tf_op jit(solution)/shard_map/all_to_all | solution.py:194
  749.5 5.6 copy.372
  765.9 39.1 %all-reduce.5 = (f32[192]{0:T(256)S(1)}, f32[192]{0:T(256)S(1)}, f32[1,2304]{1,0:T(1,128)S(1)}) all-reduce(f32[192]{0:T(256)S(1)} %dynamic-update-slice.1, f32[192]{0:T(256)S(1)} %dynamic-update-slice, f32[1,2304]{1,0:T(1,128)S(1)} %bitcast.506), channel_id=3, replica_groups=mesh['dp'=8,'seq'=4] {'dp','seq'}, use_global_device_ids=true, to_apply=%add.4 | all-reduce | flops 2688 | bytes 21504
  805.9 3.7 add_add_fusion.4
  809.6 3.0 copy.332
  812.7 88.7 %all-reduce.11.cloned.1.call-done = (f32[256,4,3,64]{0,3,2,1:T(8,128)}, f32[1,65536]{1,0:T(1,128)}, f32[1,262144]{1,0:T(1,128)}, f32[1,262144]{1,0:T(1,128)}) async-done(((f32[256,4,3,64]{0,3,2,1:T(8,128)}, f32[1,65536]{1,0:T(1,128)}, f32[1,262144]{1,0:T(1,128)}, f32[1,262144]{1,0:T(1,128)}), (f32[256,4,3,64]{0,3,2,1:T(8,128)}, f32[1,65536]{1,0:T(1,128)}, f32[1,262144]{1,0:T(1,128)}, ...) | async-done | bytes 3145744 | tf_op jit(solution)/shard_map/psum | solution.py:298
  903.3 3.5 broadcast_select_fusion.20
  908.5 3.7 dynamic_update_slice.91
  912.2 3.7 dynamic_update_slice.84
  915.8 3.9 dynamic_update_slice.98
  925.2 7.1 fusion.103
  932.3 7.1 fusion.107
  (453 shorter events, 233.6 us)
Async XLA Ops:
  55.2 4.1 copy-start.6
  69.9 133.1 %copy-start.42 = (bf16[6,256,256]{2,1,0:T(8,128)(2,1)S(1)}, bf16[6,256,256]{2,1,0:T(8,128)(2,1)}, u32[]{:S(2)}) copy-start(bf16[6,256,256]{2,1,0:T(8,128)(2,1)} %param.14) | copy-start | bytes 2359300
  203.0 115.3 %copy-start.35 = (bf16[256,4,3,64]{0,3,2,1:T(8,128)(2,1)}, bf16[256,4,3,64]{0,3,2,1:T(8,128)(2,1)S(1)}, u32[]{:S(2)}) copy-start(bf16[256,4,3,64]{0,3,2,1:T(8,128)(2,1)S(1)} %copy.259) | copy-start | bytes 1179652
  203.0 113.1 %copy-start.63 = (f32[1,256]{1,0:T(1,128)}, f32[1,256]{1,0:T(1,128)S(1)}, u32[]{:S(2)}) copy-start(f32[1,256]{1,0:T(1,128)S(1)} %get-tuple-element.328) | copy-start | bytes 3076
  203.0 115.3 %copy-start.65 = (f32[1,256]{1,0:T(1,128)}, f32[1,256]{1,0:T(1,128)S(1)}, u32[]{:S(2)}) copy-start(f32[1,256]{1,0:T(1,128)S(1)} %get-tuple-element.331) | copy-start | bytes 3076
  203.1 209.1 %copy-start.67 = (f32[1,256]{1,0:T(1,128)}, f32[1,256]{1,0:T(1,128)S(1)}, u32[]{:S(2)}) copy-start(f32[1,256]{1,0:T(1,128)S(1)} %get-tuple-element.329) | copy-start | bytes 3076
  203.3 112.8 %copy-start = (bf16[6,256,256]{1,2,0:T(8,128)(2,1)}, bf16[6,256,256]{1,2,0:T(8,128)(2,1)S(1)}, u32[]{:S(2)}) copy-start(bf16[6,256,256]{1,2,0:T(8,128)(2,1)S(1)} %copy.255) | copy-start | bytes 2359300
  203.5 2.6 copy-start.50
  203.7 6.7 copy-start.59
  203.7 6.6 copy-start.55
  213.7 33.0 %all-to-all-start = ((bf16[6,256,4,192]{1,3,0,2:T(8,128)(2,1)}), bf16[6,256,4,192]{1,3,0,2:T(8,128)(2,1)}, u32[]{:S(2)}, u32[]{:S(2)}) async-start(bf16[6,256,4,192]{1,3,0,2:T(8,128)(2,1)} %copy.263), calls=%async_computation | async-start | bytes 4718592 | tf_op jit(solution)/shard_map/all_to_all | solution.py:111
  268.5 6.7 copy-start.54
  275.2 15.5 %all-to-all-start.1 = ((bf16[4,2,49152]{2,1,0:T(2,128)(2,1)}), bf16[4,2,49152]{2,1,0:T(2,128)(2,1)S(1)}, u32[]{:S(2)}, u32[]{:S(2)}) async-start(bf16[4,2,49152]{2,1,0:T(2,128)(2,1)} %reshape.839), calls=%async_computation.1 | async-start | bytes 1572864 | tf_op jit(solution)/shard_map/all_to_all | solution.py:113
  297.3 18.9 %copy-start.3 = (f32[6,256,256]{1,2,0:T(8,128)}, f32[6,256,256]{1,2,0:T(8,128)S(1)}, u32[]{:S(2)}) copy-start(f32[6,256,256]{1,2,0:T(8,128)S(1)} %get-tuple-element.341) | copy-start | bytes 4718596
  297.3 3.5 copy-start.52
  297.5 3.4 copy-start.61
  297.5 3.3 copy-start.57
  300.9 15.3 %copy-start.29 = (f32[6,256,1024]{2,1,0:T(8,128)}, f32[6,256,1024]{2,1,0:T(8,128)S(1)}, u32[]{:S(2)}) copy-start(f32[6,256,1024]{2,1,0:T(8,128)S(1)} %get-tuple-element.342) | copy-start | bytes 18874372
  300.9 15.3 %copy-start.46 = (bf16[1024,256]{0,1:T(8,128)(2,1)S(1)}, bf16[1024,256]{0,1:T(8,128)(2,1)}, u32[]{:S(2)}) copy-start(bf16[1024,256]{0,1:T(8,128)(2,1)} %get-tuple-element.281) | copy-start | bytes 1572868
  316.2 2.0 copy-start.32
  328.4 33.0 %all-to-all-start.2 = ((bf16[6,256,4,192]{1,3,0,2:T(8,128)(2,1)}), bf16[6,256,4,192]{1,3,0,2:T(8,128)(2,1)}, u32[]{:S(2)}, u32[]{:S(2)}) async-start(bf16[6,256,4,192]{1,3,0,2:T(8,128)(2,1)} %copy.276), calls=%async_computation.2 | async-start | bytes 4718592 | tf_op jit(solution)/shard_map/all_to_all | solution.py:111
  385.8 8.0 copy-start.43
  390.1 15.2 %all-to-all-start.3 = ((bf16[4,2,49152]{2,1,0:T(2,128)(2,1)}), bf16[4,2,49152]{2,1,0:T(2,128)(2,1)S(1)}, u32[]{:S(2)}, u32[]{:S(2)}) async-start(bf16[4,2,49152]{2,1,0:T(2,128)(2,1)} %reshape.841), calls=%async_computation.3 | async-start | bytes 1572864 | tf_op jit(solution)/shard_map/all_to_all | solution.py:113
  415.5 15.1 %copy-start.44 = (bf16[6,256,256]{2,1,0:T(8,128)(2,1)S(1)}, bf16[6,256,256]{2,1,0:T(8,128)(2,1)}, u32[]{:S(2)}) copy-start(bf16[6,256,256]{2,1,0:T(8,128)(2,1)} %param.15) | copy-start | bytes 2359300
  415.5 15.1 %copy-start.47 = (bf16[1024,256]{0,1:T(8,128)(2,1)S(1)}, bf16[1024,256]{0,1:T(8,128)(2,1)}, u32[]{:S(2)}) copy-start(bf16[1024,256]{0,1:T(8,128)(2,1)} %get-tuple-element.281) | copy-start | bytes 1572868
  434.0 2.2 copy-start.73
  439.2 2.0 copy-start.12
  444.4 16.1 %all-to-all-start.4 = ((bf16[6,256,4,64]{1,3,0,2:T(8,128)(2,1)}), bf16[6,256,4,64]{1,3,0,2:T(8,128)(2,1)}, u32[]{:S(2)}, u32[]{:S(2)}) async-start(bf16[6,256,4,64]{1,3,0,2:T(8,128)(2,1)} %copy.291), calls=%async_computation.4 | async-start | bytes 1572864 | tf_op jit(solution)/shard_map/all_to_all | solution.py:186
  582.9 2.1 copy-start.36
  594.5 7.0 copy-start.8
  594.6 7.0 copy-start.71
  601.6 2.2 copy-start.75
  603.8 3.1 copy-start.53
  603.8 3.1 copy-start.58
  606.8 2.5 copy-start.62
  606.8 2.5 copy-start.4
  606.9 2.8 copy-start.13
  611.4 6.5 copy-start.72
  611.4 6.7 copy-start.64
  613.3 16.3 %all-to-all-start.6 = ((bf16[6,256,4,64]{1,3,0,2:T(8,128)(2,1)}), bf16[6,256,4,64]{1,3,0,2:T(8,128)(2,1)}, u32[]{:S(2)}, u32[]{:S(2)}) async-start(bf16[6,256,4,64]{1,3,0,2:T(8,128)(2,1)} %copy.306), calls=%async_computation.6 | async-start | bytes 1572864 | tf_op jit(solution)/shard_map/all_to_all | solution.py:186
  696.4 53.1 %all-to-all-start.7 = ((bf16[6,1024,1,192]{3,0,2,1:T(8,128)(2,1)}), bf16[6,1024,1,192]{3,0,2,1:T(8,128)(2,1)}, u32[]{:S(2)}, u32[]{:S(2)}) async-start(bf16[6,1024,1,192]{3,0,2,1:T(8,128)(2,1)} %copy.310), calls=%async_computation.7 | async-start | bytes 8388608 | tf_op jit(solution)/shard_map/all_to_all | solution.py:194
  701.3 200.0 %all-reduce.11.cloned.1.call-start = ((), (), s32[]{:S(2)}) async-start(), calls=%async_computation.8 | async-start | bytes 6291456 | tf_op jit(solution)/shard_map/psum | solution.py:298
  701.5 3.6 copy-start.15
  701.5 3.6 copy-start.45
  705.1 3.1 copy-start.5
  705.1 3.1 copy-start.68
  705.1 3.1 copy-start.76
  710.1 3.2 copy-start.20
  710.1 3.2 copy-start.26
  711.3 2.5 copy-start.24
  711.3 2.5 copy-start.28
  755.2 2.2 copy-start.1
  755.2 2.2 copy-start.51
  755.2 2.2 copy-start.56
  755.2 2.2 copy-start.66
  812.6 90.6 %copy-start.7 = (f32[1,524288]{1,0:T(1,128)S(1)}, f32[1,524288]{1,0:T(1,128)}, u32[]{:S(2)}) copy-start(f32[1,524288]{1,0:T(1,128)} %param.17) | copy-start | bytes 6291460
  908.5 3.7 copy-start.39
  908.5 7.4 copy-start.38
  912.1 7.6 copy-start.30
  912.2 7.6 copy-start.31
  919.8 3.6 copy-start.49
  921.6 3.6 copy-start.41
  925.2 7.1 copy-start.40
  939.5 2.7 copy-start.18
  (21 other events, 28.0 us)
Sparse Core Ops, SparseCore 0:
  764.7 136.5 all-reduce.10
where the time goes:
time: 962 us; the launch traced here: 949 us
  blocking collectives  226 us (23%)
  waiting for transfers between devices  217 us (23%)
  local copies, waits for them, and re-layouts  179 us (19%)
  matrix products  133 us (14%)
  other arithmetic  115 us (12%)
  between operations  48 us (5%)
  starting transfers between devices  30.6 us (3%)
    psum x1, blocking collectives, per_device(): lax.psum((owned_parts[0], owned_parts[1], owned_parts[2], owned_parts[3],...  133 us
    psum x1, waiting for transfers between devices, per_device(): lax.psum((local_sums[0], local_sums[1], local_sums[2], local_sums[3], loc...  88.7 us
    all_to_all x2, waiting for transfers between devices, block_forward(): lax.all_to_all(per_head, 'seq', split_axis=2, concat_axis=1, tiled=True)  57.1 us
    all_to_all x1, blocking collectives, block_backward(): lax.all_to_all(grad_packed, 'seq', split_axis=1, concat_axis=2, tiled=True)  53.8 us
    unnamed x1, blocking collectives  39.1 us
    unnamed x172, local copies, waits for them, and re-layouts  36.9 us
    all_to_all x1, waiting for transfers between devices, block_backward(): lax.all_to_all(grad_packed, 'seq', split_axis=1, concat_axis=2, tiled=True)  34 us
    convert_element_type x2, other arithmetic, block_forward(): hidden_units = jax.nn.gelu(before, approximate=False).astype(jnp.bfloat16)  30.4 us
  transfers between devices with their start and end apart: 8, of which 8 were waited for; matrix products, arithmetic and copies ran while one was open for 3% of the time, Pallas kernels for 0%

commit v1 on v0

--- a/solution.py
+++ b/solution.py
@@ -191,8 +191,11 @@
         tiled=True,
     )
     grad_packed = lax.map(attend_single_back, (packed, log_total, grad_heads))
-    projected_gradient = lax.all_to_all(
-        grad_packed, "seq", split_axis=1, concat_axis=2, tiled=True
+    projected_gradient = jnp.concatenate(
+        lax.all_to_all(
+            jnp.stack(jnp.split(grad_packed, lax.axis_size("seq"), axis=1)), "seq", 0, 0
+        ),
+        axis=2,
     ).reshape(seq_count, quarter, 3 * features)
     grad_joined = jnp.einsum(
         "tck,tcp->kp", normalized_input, projected_gradient, preferred_element_type=jnp.float32

time: 962 us -> 898 us (0.933)
  local copies, waits for them, and re-layouts: 179 us -> 156 us
  blocking collectives: 226 us -> 203 us
  waiting for transfers between devices: 217 us -> 198 us
    all_to_all x1, blocking collectives: 53.8 us -> 31 us  [block_backward(): lax.all_to_all(jnp.stack(jnp.split(grad_packed, lax.axis_size('seq'), axi...]
    all_to_all x1, waiting for transfers between devices: 34 us -> 14.5 us  [block_backward(): lax.all_to_all(jnp.stack(jnp.split(grad_packed, lax.axis_size('seq'), axi...]
    all_to_all x4 -> x2, local copies, waits for them, and re-layouts: 15.5 us -> 2.04 us  [block_backward(): lax.all_to_all(jnp.stack(jnp.split(grad_packed, lax.axis_size('seq'), axi...]
    while x2 -> x0, local copies, waits for them, and re-layouts: 13.1 us -> none  [block_backward(): grad_packed = lax.map(attend_single_back, (packed, log_total, grad_heads))]
where the time goes in v1:
time: 898 us; the launch traced here: 886 us
  blocking collectives  203 us (23%)
  waiting for transfers between devices  198 us (22%)
  local copies, waits for them, and re-layouts  156 us (17%)
  matrix products  133 us (15%)
  other arithmetic  117 us (13%)
  between operations  48 us (5%)
  starting transfers between devices  30.3 us (3%)
    psum x1, blocking collectives, per_device(): lax.psum((owned_parts[0], owned_parts[1], owned_parts[2], owned_parts[3],...  133 us
    psum x1, waiting for transfers between devices, per_device(): lax.psum((local_sums[0], local_sums[1], local_sums[2], local_sums[3], loc...  88.7 us
    all_to_all x2, waiting for transfers between devices, block_forward(): lax.all_to_all(per_head, 'seq', split_axis=2, concat_axis=1, tiled=True)  57.1 us
    unnamed x1, blocking collectives  39.1 us
    unnamed x172, local copies, waits for them, and re-layouts  37.7 us
    all_to_all x1, blocking collectives, block_backward(): lax.all_to_all(jnp.stack(jnp.split(grad_packed, lax.axis_size('seq'), axi...  31 us
    convert_element_type x2, other arithmetic, block_forward(): hidden_units = jax.nn.gelu(before, approximate=False).astype(jnp.bfloat16)  30.3 us
    squeeze x24, local copies, waits for them, and re-layouts, attend_items(): attention_output, log_total = lax.map(attend_single, packed_items)  24.6 us
  transfers between devices with their start and end apart: 8, of which 8 were waited for; matrix products, arithmetic and copies ran while one was open for 3% of the time, Pallas kernels for 0%

profile of v1, /device:TPU:0, one launch (start us, length us, event | category | flops | bytes accessed | tf_op | source)
XLA Modules:
  0.0 886.4 jit_solution(13015171303782707043)
XLA Ops:
  40.8 13.1 %fusion.104 = (f32[262144]{0:T(1024)S(1)}, f32[262144]{0:T(1024)}) fusion(pred[]{:T(512)S(6)} %eq.113, f32[1,524288]{1,0:T(1,128)} %param.17, s32[]{:T(128)S(6)} %select_n.271, s32[]{:T(128)S(6)} %select_n.267, pred[]{:T(512)S(6)} %eq.108), kind=kLoop, calls=%fused_computation.229 | loop fusion | flops 524288 | bytes 4194314 | tf_op jit(solution)/shard_map/jit(_where)/select_n | solution.py:249
  56.9 2.4 select_n.269
  59.3 3.5 fusion.134
  69.9 132.7 %all-reduce.12 = (bf16[256,256]{1,0:T(8,128)(2,1)S(1)}, bf16[256,256]{1,0:T(8,128)(2,1)S(1)}, bf16[256,256]{1,0:T(8,128)(2,1)S(1)}, f32[9,256]{1,0:T(8,128)S(1)}...) all-reduce(f32[256,256]{1,0:T(8,128)} %select_n.261, ...), channel_id=1, replica_groups=mesh['dp'=8,'seq'=4] {'dp'}, use_global_device_ids=true, to_apply=%region_5.6 | all-reduce | flops 788736 | bytes 4737024 | tf_op jit(solution)/shard_map/psum | solution.py:250
  203.8 2.4 convolution_convert_fusion.1
  206.1 4.3 copy.286
  210.4 3.3 copy.287
  213.7 4.5 all-to-all-start
  218.2 28.5 %all-to-all-done = bf16[6,256,4,192]{1,3,0,2:T(8,128)(2,1)} async-done(((bf16[6,256,4,192]{1,3,0,2:T(8,128)(2,1)}), bf16[6,256,4,192]{1,3,0,2:T(8,128)(2,1)}, u32[]{:S(2)}, u32[]{:S(2)}) %all-to-all-start) | async-done | bytes 2359328 | tf_op jit(solution)/shard_map/all_to_all | solution.py:111
  246.7 3.4 copy.400
  250.2 18.3 %while.44 = (s32[]{:T(128)}, bf16[6,1024,1,64]{1,3,2,0:T(8,128)(2,1)S(1)}, f32[6,1,1024]{2,1,0:T(1,128)S(1)}, bf16[6,1024,1,192]{1,3,2,0:T(8,128)(2,1)}, s32[]{:T(128)}) while((s32[]{:T(128)}, bf16[6,1024,1,64]{1,3,2,0:T(8,128)(2,1)S(1)}, f32[6,1,1024]{2,1,0:T(1,128)S(1)}, bf16[6,1024,1,192]{1,3,2,0:T(8,128)(2,1)}, s32[]{:T(128)}) %tuple.171), condition=%wide.region_9.10_spmd, body=%wide.region_6.9_spmd.sunk | while | flops 284228608 | bytes 13934665 | solution.py:72
  268.6 2.5 copy.290
  271.1 4.2 reshape.837
  275.3 3.9 all-to-all-start.1
  279.2 11.5 %all-to-all-done.1 = bf16[4,2,49152]{2,1,0:T(2,128)(2,1)S(1)} async-done(((bf16[4,2,49152]{2,1,0:T(2,128)(2,1)}), bf16[4,2,49152]{2,1,0:T(2,128)(2,1)S(1)}, u32[]{:S(2)}, u32[]{:S(2)}) %all-to-all-start.1) | async-done | bytes 786464 | tf_op jit(solution)/shard_map/all_to_all | solution.py:113
  290.8 2.5 reshape.838
  293.3 2.6 copy.390
  298.1 2.9 fusion.88
  301.0 15.2 %multiply_convert_fusion.3 = (bf16[6,256,1024]{2,1,0:T(8,128)(2,1)S(1)}, f32[6,256,1024]{2,1,0:T(8,128)}) fusion(f32[6,256,1024]{2,1,0:T(8,128)S(1)} %get-tuple-element.350, f32[1024]{0:T(1024)S(1)} %bitcast.522, u8[256,1024]{1,0:T(8,128)(4,1)S(1)} %get-tuple-element.217, u8[256,1024]{1,0:T(8,128)(4,1)S(1)} %get-tuple-element.216), kind=kLoop, calls=%fused_computation.130 | loop fusion | flops 111673344 | bytes 16257024 | tf_op jit(solution)/shard_map/convert_element_type | solution.py:125
  318.5 2.4 convolution_convert_fusion
  320.9 4.3 copy.299
  325.2 3.3 copy.300
  328.4 4.5 all-to-all-start.2
  332.9 28.5 %all-to-all-done.2 = bf16[6,256,4,192]{1,3,0,2:T(8,128)(2,1)} async-done(((bf16[6,256,4,192]{1,3,0,2:T(8,128)(2,1)}), bf16[6,256,4,192]{1,3,0,2:T(8,128)(2,1)}, u32[]{:S(2)}, u32[]{:S(2)}) %all-to-all-start.2) | async-done | bytes 2359328 | tf_op jit(solution)/shard_map/all_to_all | solution.py:111
  361.5 3.4 copy.401
  365.0 18.3 %while.45 = (s32[]{:T(128)}, bf16[6,1024,1,64]{1,3,2,0:T(8,128)(2,1)S(1)}, f32[6,1,1024]{2,1,0:T(1,128)S(1)}, bf16[6,1024,1,192]{1,3,2,0:T(8,128)(2,1)}, s32[]{:T(128)}) while((s32[]{:T(128)}, bf16[6,1024,1,64]{1,3,2,0:T(8,128)(2,1)S(1)}, f32[6,1,1024]{2,1,0:T(1,128)S(1)}, bf16[6,1024,1,192]{1,3,2,0:T(8,128)(2,1)}, s32[]{:T(128)}) %tuple.173), condition=%wide.region_20.21_spmd, body=%wide.region_17.20_spmd.sunk | while | flops 284228608 | bytes 13934665 | solution.py:72
  383.4 2.5 copy.303
  385.9 4.3 reshape.839
  390.2 3.7 all-to-all-start.3
  395.0 10.4 %all-to-all-done.3 = bf16[4,2,49152]{2,1,0:T(2,128)(2,1)S(1)} async-done(((bf16[4,2,49152]{2,1,0:T(2,128)(2,1)}), bf16[4,2,49152]{2,1,0:T(2,128)(2,1)S(1)}, u32[]{:S(2)}, u32[]{:S(2)}) %all-to-all-start.3) | async-done | bytes 786464 | tf_op jit(solution)/shard_map/all_to_all | solution.py:113
  405.4 2.5 reshape.840
  407.9 2.6 copy.392
  412.7 2.9 fusion.89
  415.6 15.1 %multiply_convert_fusion.2 = (bf16[6,256,1024]{2,1,0:T(8,128)(2,1)}, f32[6,256,1024]{2,1,0:T(8,128)S(1)}) fusion(f32[6,256,1024]{2,1,0:T(8,128)S(1)} %get-tuple-element.353, f32[1024]{0:T(1024)S(1)} %bitcast.524, u8[256,1024]{1,0:T(8,128)(4,1)S(1)} %get-tuple-element.215, u8[256,1024]{1,0:T(8,128)(4,1)S(1)} %get-tuple-element.214), kind=kLoop, calls=%fused_computation.117 | loop fusion | flops 111673344 | bytes 16257024 | tf_op jit(solution)/shard_map/convert_element_type | solution.py:125
  430.7 3.4 convert_reduce_fusion.1
  434.1 2.2 fusion.168
  436.3 3.0 copy.312
  444.5 4.4 all-to-all-start.4
  448.9 11.7 %all-to-all-done.4 = bf16[6,256,4,64]{1,3,0,2:T(8,128)(2,1)} async-done(((bf16[6,256,4,64]{1,3,0,2:T(8,128)(2,1)}), bf16[6,256,4,64]{1,3,0,2:T(8,128)(2,1)}, u32[]{:S(2)}, u32[]{:S(2)}) %all-to-all-start.4) | async-done | bytes 786464 | tf_op jit(solution)/shard_map/all_to_all | solution.py:186
  464.4 52.6 %while.46 = (s32[]{:T(128)}, bf16[6,1024,1,192]{1,3,2,0:T(8,128)(2,1)}, bf16[6,1024,1,192]{1,3,2,0:T(8,128)(2,1)}, f32[6,1,1024]{2,1,0:T(1,128)S(1)}, bf16[6,1024,1,64]{1,3,2,0:T(8,128)(2,1)}, /*index=5*/s32[]{:T(128)}) while((s32[]{:T(128)}, bf16[6,1024,1,192]{1,3,2,0:T(8,128)(2,1)}, bf16[6,1024,1,192]{1,3,2,0:T(8,128)(2,1)}, ...), condition=%wide.region_27.28_spmd, body=%wide.region_25.27_spmd.sunk | while | flops 683080704 | bytes 34362956 | solution.py:193
  519.1 31.0 %all_to_all.112 = bf16[4,6,256,1,192]{2,4,1,3,0:T(8,128)(2,1)S(1)} all-to-all(bf16[4,6,256,1,192]{2,4,1,3,0:T(8,128)(2,1)S(1)} %pad_maximum_fusion), channel_id=1, replica_groups=mesh['dp'=8,'seq'=4] {'seq'}, dimensions={0} | all-to-all | bytes 4718592 | tf_op jit(solution)/shard_map/all_to_all | solution.py:195
  553.0 3.0 copy.326
  560.6 7.0 convert_reduce_fusion
  567.6 2.2 fusion.170
  569.8 3.0 copy.329
  572.9 2.5 multiply_reduce_fusion.2
  579.2 4.6 all-to-all-start.6
  584.1 4.2 multiply_reduce_fusion.5
  588.3 3.0 copy.359
  591.5 4.0 all-to-all-done.6
  599.3 56.6 %while.47 = (s32[]{:T(128)}, bf16[6,1024,1,192]{1,3,2,0:T(8,128)(2,1)}, bf16[6,1024,1,192]{1,3,2,0:T(8,128)(2,1)}, f32[6,1,1024]{2,1,0:T(1,128)}, bf16[6,1024,1,64]{1,3,2,0:T(8,128)(2,1)}, /*index=5*/s32[]{:T(128)}) while((s32[]{:T(128)}, bf16[6,1024,1,192]{1,3,2,0:T(8,128)(2,1)}, bf16[6,1024,1,192]{1,3,2,0:T(8,128)(2,1)}, ...), condition=%wide.region_34.35_spmd, body=%wide.region_32.34_spmd.sunk | while | flops 683080704 | bytes 34362956 | solution.py:193
  659.4 4.5 all-to-all-start.7
  664.2 3.5 convolution_bitcast_fusion
  678.0 14.5 %all-to-all-done.7 = bf16[4,6,256,1,192]{2,4,1,3,0:T(8,128)(2,1)} async-done(((bf16[4,6,256,1,192]{2,4,1,3,0:T(8,128)(2,1)}), bf16[4,6,256,1,192]{2,4,1,3,0:T(8,128)(2,1)}, u32[]{:S(2)}, u32[]{:S(2)}) %all-to-all-start.7) | async-done | bytes 2359328 | tf_op jit(solution)/shard_map/all_to_all | solution.py:195
  702.9 39.1 %all-reduce.5 = (f32[192]{0:T(256)S(1)}, f32[192]{0:T(256)S(1)}, f32[1,2304]{1,0:T(1,128)S(1)}) all-reduce(f32[192]{0:T(256)S(1)} %dynamic-update-slice.1, f32[192]{0:T(256)S(1)} %dynamic-update-slice, f32[1,2304]{1,0:T(1,128)S(1)} %bitcast.527), channel_id=3, replica_groups=mesh['dp'=8,'seq'=4] {'dp','seq'}, use_global_device_ids=true, to_apply=%add.4 | all-reduce | flops 2688 | bytes 21504
  742.9 3.7 add_add_fusion.4
  746.6 3.0 copy.360
  749.7 88.7 %all-reduce.11.cloned.1.call-done = (f32[256,4,3,64]{0,3,2,1:T(8,128)}, f32[1,65536]{1,0:T(1,128)}, f32[1,262144]{1,0:T(1,128)}, f32[1,262144]{1,0:T(1,128)}) async-done(((f32[256,4,3,64]{0,3,2,1:T(8,128)}, f32[1,65536]{1,0:T(1,128)}, f32[1,262144]{1,0:T(1,128)}, f32[1,262144]{1,0:T(1,128)}), (f32[256,4,3,64]{0,3,2,1:T(8,128)}, f32[1,65536]{1,0:T(1,128)}, f32[1,262144]{1,0:T(1,128)}, ...) | async-done | bytes 3145744 | tf_op jit(solution)/shard_map/psum | solution.py:301
  840.3 3.5 broadcast_select_fusion.20
  845.5 3.7 dynamic_update_slice.91
  849.2 3.7 dynamic_update_slice.84
  852.8 3.9 dynamic_update_slice.98
  862.1 7.1 fusion.103
  869.2 7.1 fusion.107
  (453 shorter events, 228.6 us)
Async XLA Ops:
  55.2 4.1 copy-start.6
  69.9 133.1 %copy-start.42 = (bf16[6,256,256]{2,1,0:T(8,128)(2,1)S(1)}, bf16[6,256,256]{2,1,0:T(8,128)(2,1)}, u32[]{:S(2)}) copy-start(bf16[6,256,256]{2,1,0:T(8,128)(2,1)} %param.14) | copy-start | bytes 2359300
  203.0 115.5 %copy-start.35 = (bf16[256,4,3,64]{0,3,2,1:T(8,128)(2,1)}, bf16[256,4,3,64]{0,3,2,1:T(8,128)(2,1)S(1)}, u32[]{:S(2)}) copy-start(bf16[256,4,3,64]{0,3,2,1:T(8,128)(2,1)S(1)} %copy.283) | copy-start | bytes 1179652
  203.0 113.2 %copy-start.63 = (f32[1,256]{1,0:T(1,128)}, f32[1,256]{1,0:T(1,128)S(1)}, u32[]{:S(2)}) copy-start(f32[1,256]{1,0:T(1,128)S(1)} %get-tuple-element.336) | copy-start | bytes 3076
  203.0 115.4 %copy-start.65 = (f32[1,256]{1,0:T(1,128)}, f32[1,256]{1,0:T(1,128)S(1)}, u32[]{:S(2)}) copy-start(f32[1,256]{1,0:T(1,128)S(1)} %get-tuple-element.339) | copy-start | bytes 3076
  203.1 209.2 %copy-start.67 = (f32[1,256]{1,0:T(1,128)}, f32[1,256]{1,0:T(1,128)S(1)}, u32[]{:S(2)}) copy-start(f32[1,256]{1,0:T(1,128)S(1)} %get-tuple-element.337) | copy-start | bytes 3076
  203.3 112.9 %copy-start = (bf16[6,256,256]{1,2,0:T(8,128)(2,1)}, bf16[6,256,256]{1,2,0:T(8,128)(2,1)S(1)}, u32[]{:S(2)}) copy-start(bf16[6,256,256]{1,2,0:T(8,128)(2,1)S(1)} %copy.279) | copy-start | bytes 2359300
  203.5 2.6 copy-start.50
  203.7 6.7 copy-start.59
  203.7 6.6 copy-start.55
  213.7 33.0 %all-to-all-start = ((bf16[6,256,4,192]{1,3,0,2:T(8,128)(2,1)}), bf16[6,256,4,192]{1,3,0,2:T(8,128)(2,1)}, u32[]{:S(2)}, u32[]{:S(2)}) async-start(bf16[6,256,4,192]{1,3,0,2:T(8,128)(2,1)} %copy.287), calls=%async_computation | async-start | bytes 4718592 | tf_op jit(solution)/shard_map/all_to_all | solution.py:111
  268.6 6.7 copy-start.54
  275.3 15.5 %all-to-all-start.1 = ((bf16[4,2,49152]{2,1,0:T(2,128)(2,1)}), bf16[4,2,49152]{2,1,0:T(2,128)(2,1)S(1)}, u32[]{:S(2)}, u32[]{:S(2)}) async-start(bf16[4,2,49152]{2,1,0:T(2,128)(2,1)} %reshape.837), calls=%async_computation.1 | async-start | bytes 1572864 | tf_op jit(solution)/shard_map/all_to_all | solution.py:113
  297.4 18.9 %copy-start.3 = (f32[6,256,256]{1,2,0:T(8,128)}, f32[6,256,256]{1,2,0:T(8,128)S(1)}, u32[]{:S(2)}) copy-start(f32[6,256,256]{1,2,0:T(8,128)S(1)} %get-tuple-element.349) | copy-start | bytes 4718596
  297.4 3.5 copy-start.52
  297.6 3.4 copy-start.61
  297.7 3.3 copy-start.57
  301.0 15.3 %copy-start.29 = (f32[6,256,1024]{2,1,0:T(8,128)}, f32[6,256,1024]{2,1,0:T(8,128)S(1)}, u32[]{:S(2)}) copy-start(f32[6,256,1024]{2,1,0:T(8,128)S(1)} %get-tuple-element.350) | copy-start | bytes 18874372
  301.0 15.3 %copy-start.46 = (bf16[1024,256]{0,1:T(8,128)(2,1)S(1)}, bf16[1024,256]{0,1:T(8,128)(2,1)}, u32[]{:S(2)}) copy-start(bf16[1024,256]{0,1:T(8,128)(2,1)} %get-tuple-element.281) | copy-start | bytes 1572868
  316.3 2.0 copy-start.32
  328.4 33.0 %all-to-all-start.2 = ((bf16[6,256,4,192]{1,3,0,2:T(8,128)(2,1)}), bf16[6,256,4,192]{1,3,0,2:T(8,128)(2,1)}, u32[]{:S(2)}, u32[]{:S(2)}) async-start(bf16[6,256,4,192]{1,3,0,2:T(8,128)(2,1)} %copy.300), calls=%async_computation.2 | async-start | bytes 4718592 | tf_op jit(solution)/shard_map/all_to_all | solution.py:111
  385.9 8.0 copy-start.43
  390.2 15.2 %all-to-all-start.3 = ((bf16[4,2,49152]{2,1,0:T(2,128)(2,1)}), bf16[4,2,49152]{2,1,0:T(2,128)(2,1)S(1)}, u32[]{:S(2)}, u32[]{:S(2)}) async-start(bf16[4,2,49152]{2,1,0:T(2,128)(2,1)} %reshape.839), calls=%async_computation.3 | async-start | bytes 1572864 | tf_op jit(solution)/shard_map/all_to_all | solution.py:113
  415.5 15.1 %copy-start.44 = (bf16[6,256,256]{2,1,0:T(8,128)(2,1)S(1)}, bf16[6,256,256]{2,1,0:T(8,128)(2,1)}, u32[]{:S(2)}) copy-start(bf16[6,256,256]{2,1,0:T(8,128)(2,1)} %param.15) | copy-start | bytes 2359300
  415.6 15.1 %copy-start.47 = (bf16[1024,256]{0,1:T(8,128)(2,1)S(1)}, bf16[1024,256]{0,1:T(8,128)(2,1)}, u32[]{:S(2)}) copy-start(bf16[1024,256]{0,1:T(8,128)(2,1)} %get-tuple-element.281) | copy-start | bytes 1572868
  434.1 2.2 copy-start.73
  439.3 2.0 copy-start.12
  444.5 16.1 %all-to-all-start.4 = ((bf16[6,256,4,64]{1,3,0,2:T(8,128)(2,1)}), bf16[6,256,4,64]{1,3,0,2:T(8,128)(2,1)}, u32[]{:S(2)}, u32[]{:S(2)}) async-start(bf16[6,256,4,64]{1,3,0,2:T(8,128)(2,1)} %copy.315), calls=%async_computation.4 | async-start | bytes 1572864 | tf_op jit(solution)/shard_map/all_to_all | solution.py:186
  550.3 2.7 copy-start.33
  560.5 7.0 copy-start.8
  560.5 7.0 copy-start.71
  567.6 2.2 copy-start.75
  569.8 3.1 copy-start.53
  569.8 3.1 copy-start.58
  572.8 2.5 copy-start.62
  572.8 2.5 copy-start.4
  572.8 2.8 copy-start.13
  577.4 6.4 copy-start.72
  577.4 6.7 copy-start.64
  579.2 16.3 %all-to-all-start.6 = ((bf16[6,256,4,64]{1,3,0,2:T(8,128)(2,1)}), bf16[6,256,4,64]{1,3,0,2:T(8,128)(2,1)}, u32[]{:S(2)}, u32[]{:S(2)}) async-start(bf16[6,256,4,64]{1,3,0,2:T(8,128)(2,1)} %copy.332), calls=%async_computation.6 | async-start | bytes 1572864 | tf_op jit(solution)/shard_map/all_to_all | solution.py:186
  659.4 33.1 %all-to-all-start.7 = ((bf16[4,6,256,1,192]{2,4,1,3,0:T(8,128)(2,1)}), bf16[4,6,256,1,192]{2,4,1,3,0:T(8,128)(2,1)}, u32[]{:S(2)}, u32[]{:S(2)}) async-start(bf16[4,6,256,1,192]{2,4,1,3,0:T(8,128)(2,1)} %pad_maximum_fusion.1), calls=%async_computation.7 | async-start | bytes 4718592 | tf_op jit(solution)/shard_map/all_to_all | solution.py:195
  664.0 174.4 %all-reduce.11.cloned.1.call-start = ((), (), s32[]{:S(2)}) async-start(), calls=%async_computation.8 | async-start | bytes 6291456 | tf_op jit(solution)/shard_map/psum | solution.py:301
  664.2 3.6 copy-start.15
  664.2 3.6 copy-start.45
  667.8 3.1 copy-start.5
  667.8 3.1 copy-start.68
  667.8 3.1 copy-start.76
  672.8 3.2 copy-start.20
  672.8 3.2 copy-start.26
  673.9 2.5 copy-start.24
  673.9 2.5 copy-start.28
  678.0 16.4 %copy-start.1 = (bf16[6,256,256]{1,2,0:T(8,128)(2,1)S(1)}, bf16[6,256,256]{1,2,0:T(8,128)(2,1)}, u32[]{:S(2)}) copy-start(bf16[6,256,256]{1,2,0:T(8,128)(2,1)} %copy-done) | copy-start | bytes 2359300
  678.0 16.4 %copy-start.51 = (f32[6,256]{1,0:T(8,128)S(1)}, f32[6,256]{1,0:T(8,128)}, u32[]{:S(2)}) copy-start(f32[6,256]{1,0:T(8,128)} %copy-done.50) | copy-start | bytes 18436
  678.0 16.4 %copy-start.56 = (f32[6,256]{1,0:T(8,128)S(1)}, f32[6,256]{1,0:T(8,128)}, u32[]{:S(2)}) copy-start(f32[6,256]{1,0:T(8,128)} %copy-done.55) | copy-start | bytes 18436
  678.0 16.4 %copy-start.66 = (f32[1,256]{1,0:T(1,128)S(1)}, f32[1,256]{1,0:T(1,128)}, u32[]{:S(2)}) copy-start(f32[1,256]{1,0:T(1,128)} %copy-done.65) | copy-start | bytes 3076
  749.7 90.6 %copy-start.7 = (f32[1,524288]{1,0:T(1,128)S(1)}, f32[1,524288]{1,0:T(1,128)}, u32[]{:S(2)}) copy-start(f32[1,524288]{1,0:T(1,128)} %param.17) | copy-start | bytes 6291460
  845.5 3.7 copy-start.39
  845.5 7.4 copy-start.38
  849.1 7.6 copy-start.30
  849.2 7.6 copy-start.31
  856.8 3.6 copy-start.49
  858.6 3.6 copy-start.41
  862.1 7.1 copy-start.40
  876.5 2.7 copy-start.18
  (21 other events, 27.1 us)
Sparse Core Ops, SparseCore 0:
  701.7 136.5 all-reduce.10
